TPU v7x, 128 devices: a whole 4x4x4 slice. The times are simulated.
128 devices in a mesh: model: 1, replica: 64 (over z, y, x), fsdp: 2 (over core).
Axes of the slice: x: 4, y: 4, z: 4, core: 2. Of those that a mesh axis runs over, the one named last changes fastest.
Arguments:
- x_in: bfloat16 [4, 65536, 1024], P(None, ('model', 'replica', 'fsdp'))
- dy_out: bfloat16 [4, 65536, 1024], P(None, ('model', 'replica', 'fsdp'))
- lengths: int32 [4, 128], P(None, ('model', 'replica', 'fsdp'))
- w_up: bfloat16 [1, 1024, 4096], P(None, ('model', 'fsdp'))
- w_down: bfloat16 [1, 4096, 1024], P(None, ('model', 'fsdp'))
Outputs:
- output 1: float32 [1, 1024, 4096], P(None, ('model', 'fsdp'))
- output 2: float32 [1, 4096, 1024], P(None, ('model', 'fsdp'))
All inputs are finite; a program needn't handle non-finite values.
Results may differ from a plain program's by a relative error of at most 0.001.
Values are sent between devices in bfloat16 or wider.
A program may use at most 1 GiB of HBM per device.

v0:
```python
import jax
import jax.numpy as jnp
from jax import lax
from jax.sharding import PartitionSpec as P, NamedSharding


def gather_full(w_shard):
    return lax.all_gather(w_shard, "fsdp", axis=0, tiled=True)


def solution(mesh):
    tok_spec = P(None, ("model", "replica", "fsdp"), None)
    len_spec = P(None, ("model", "replica", "fsdp"))
    w_spec = P(None, ("model", "fsdp"), None)

    def device_grads(x_in, dy_out, lengths, w_up, w_down):
        tok_dev = x_in.shape[1]
        n_layers = w_up.shape[0]
        token_mask = jnp.arange(tok_dev)[None, :] < lengths

        def micro_step(acc_pair, micro_in):
            x_cur, dy_cur, mask_cur = micro_in
            saved_acts = []
            for layer_idx in range(n_layers):
                up_full = gather_full(w_up[layer_idx])
                hidden = jnp.dot(x_cur, up_full, preferred_element_type=jnp.float32).astype(jnp.bfloat16)
                saved_acts.append((x_cur, hidden))
                if layer_idx + 1 < n_layers:
                    down_full = gather_full(w_down[layer_idx])
                    act_bf = jax.nn.gelu(hidden.astype(jnp.float32)).astype(jnp.bfloat16)
                    x_cur = (x_cur.astype(jnp.float32) + jnp.dot(act_bf, down_full, preferred_element_type=jnp.float32)).astype(jnp.bfloat16)
            grad_x = jnp.where(mask_cur[:, None], dy_cur, jnp.zeros_like(dy_cur))
            new_up = list(acc_pair[0])
            new_down = list(acc_pair[1])
            for layer_idx in reversed(range(n_layers)):
                x_prev, hidden = saved_acts[layer_idx]
                down_full = gather_full(w_down[layer_idx])
                act_f32, gelu_vjp = jax.vjp(jax.nn.gelu, hidden.astype(jnp.float32))
                act_bf = act_f32.astype(jnp.bfloat16)
                grad_act = jnp.einsum("td,fd->tf", grad_x, down_full, preferred_element_type=jnp.float32)
                grad_hid = gelu_vjp(grad_act)[0].astype(jnp.bfloat16)
                gw_down = jnp.einsum("tf,td->fd", act_bf, grad_x, preferred_element_type=jnp.float32)
                gw_up = jnp.einsum("td,tf->df", x_prev, grad_hid, preferred_element_type=jnp.float32)
                if layer_idx > 0:
                    up_full = gather_full(w_up[layer_idx])
                    grad_x = (grad_x.astype(jnp.float32) + jnp.einsum("tf,df->td", grad_hid, up_full, preferred_element_type=jnp.float32)).astype(jnp.bfloat16)
                new_up[layer_idx] = new_up[layer_idx] + lax.psum_scatter(gw_up, "fsdp", scatter_dimension=0, tiled=True)
                new_down[layer_idx] = new_down[layer_idx] + lax.psum_scatter(gw_down, "fsdp", scatter_dimension=0, tiled=True)
            return (tuple(new_up), tuple(new_down)), None

        init_up = tuple(jnp.zeros(w_up.shape[1:], jnp.float32) for layer_idx in range(n_layers))
        init_down = tuple(jnp.zeros(w_down.shape[1:], jnp.float32) for layer_idx in range(n_layers))
        (acc_up, acc_down), _ = lax.scan(micro_step, (init_up, init_down), (x_in, dy_out, token_mask))
        grad_up = lax.psum(jnp.stack(acc_up), "replica")
        grad_down = lax.psum(jnp.stack(acc_down), "replica")
        return grad_up, grad_down

    return jax.shard_map(device_grads, mesh=mesh, in_specs=(tok_spec, tok_spec, len_spec, w_spec, w_spec), out_specs=(w_spec, w_spec), check_vma=False)
```

profile of v0, /device:TPU:0, one launch (start us, length us, event | category | flops | bytes accessed | tf_op | source)
XLA Modules:
  0.0 823.8 jit_solution(13531102769152129555)
XLA Ops:
  8.7 573.7 %while.15 = (s32[]{:T(128)}, f32[512,4096]{1,0:T(8,128)}, f32[2048,1024]{1,0:T(8,128)}, bf16[4,512,1024]{2,1,0:T(8,128)(2,1)}, pred[4,512]{1,0:T(4,128)(4,1)S(1)...) while((s32[]{:T(128)}, f32[512,4096]{1,0:T(8,128)}, ...), condition=%wide.region_3.4_spmd.clone, body=%wide.region_0.3_spmd.clone.sunk | while | flops 17256415232 | bytes 343937280 | solution.py:53
  10.3 26.9 %all-gather.11.cloned.1.call-done = bf16[1,1024,4096]{2,1,0:T(8,128)(2,1)} async-done(((bf16[1,512,4096]{2,1,0:T(8,128)(2,1)}), bf16[1,1024,4096]{2,1,0:T(8,128)(2,1)}) %all-gather.11.cloned.1.call-update) | async-done | bytes 8388624 | tf_op jit(solution)/shard_map/while/body/eval_jaxpr/all_gather | solution.py:8
  47.4 16.4 %all-gather.13.cloned.1.call-done = bf16[1,4096,1024]{2,1,0:T(8,128)(2,1)} async-done(((bf16[1,2048,1024]{2,1,0:T(8,128)(2,1)}), bf16[1,4096,1024]{2,1,0:T(8,128)(2,1)}) %all-gather.13.cloned.1.call-update) | async-done | bytes 8388624 | tf_op jit(solution)/shard_map/while/body/eval_jaxpr/all_gather | solution.py:8
  63.8 18.2 %fusion.66 = f32[1024,4096]{1,0:T(8,128)} fusion(bf16[512,4096]{1,0:T(8,128)(2,1)} %fusion.65, bf16[4,512,1024]{2,1,0:T(8,128)(2,1)} %get-tuple-element.223, s32[]{:T(128)} %get-tuple-element.210, bf16[1,4096,1024]{2,1,0:T(8,128)(2,1)} %all-gather.13.cloned.1.call-done, bf16[4,512,1024]{2,1,0:T(8,128)(2,1)} %get-tuple-element.225, ...), kind=kOutput, calls=%fused_computation.27.clone.1 | convolution fusion | flops 8634499072 | bytes 31458816 | tf_op jit(solution)/shard_map/while/body/eval_jaxpr/td,tf->df/dot_general | solution.py:43
  82.0 14.8 %fusion.67 = f32[4096,1024]{1,0:T(8,128)} fusion(bf16[512,4096]{1,0:T(8,128)(2,1)} %fusion.65, bf16[4,512,1024]{2,1,0:T(8,128)(2,1)} %get-tuple-element.225, s32[]{:T(128)} %get-tuple-element.210, pred[512]{0:T(512)(128)(4,1)S(1)} %dynamic-slice_reduce_fusion.2), kind=kOutput, calls=%fused_computation.22.clone.1 | convolution fusion | flops 4316463104 | bytes 22021120 | tf_op jit(solution)/shard_map/while/body/eval_jaxpr/tf,td->fd/dot_general | solution.py:42
  96.8 13.9 %reduce-scatter.3.cloned.1.call-done = f32[512,4096]{1,0:T(8,128)} async-done(((f32[1024,4096]{1,0:T(8,128)}), f32[512,4096]{1,0:T(8,128)}) %reduce-scatter.3.cloned.1.call-update) | async-done | bytes 8388624 | tf_op jit(solution)/shard_map/while/body/eval_jaxpr/reduce_scatter | solution.py:47
  119.9 21.7 %reduce-scatter.5.cloned.1.call-done = f32[2048,1024]{1,0:T(8,128)} async-done(((f32[4096,1024]{1,0:T(8,128)}), f32[2048,1024]{1,0:T(8,128)}) %reduce-scatter.5.cloned.1.call-update) | async-done | bytes 8388624 | tf_op jit(solution)/shard_map/while/body/eval_jaxpr/reduce_scatter | solution.py:48
  152.6 25.8 %all-gather.11.cloned.1.call-done = bf16[1,1024,4096]{2,1,0:T(8,128)(2,1)} async-done(((bf16[1,512,4096]{2,1,0:T(8,128)(2,1)}), bf16[1,1024,4096]{2,1,0:T(8,128)(2,1)}) %all-gather.11.cloned.1.call-update) | async-done | bytes 8388624 | tf_op jit(solution)/shard_map/while/body/eval_jaxpr/all_gather | solution.py:8
  188.6 16.2 %all-gather.13.cloned.1.call-done = bf16[1,4096,1024]{2,1,0:T(8,128)(2,1)} async-done(((bf16[1,2048,1024]{2,1,0:T(8,128)(2,1)}), bf16[1,4096,1024]{2,1,0:T(8,128)(2,1)}) %all-gather.13.cloned.1.call-update) | async-done | bytes 8388624 | tf_op jit(solution)/shard_map/while/body/eval_jaxpr/all_gather | solution.py:8
  204.8 18.2 %fusion.66 = f32[1024,4096]{1,0:T(8,128)} fusion(bf16[512,4096]{1,0:T(8,128)(2,1)} %fusion.65, bf16[4,512,1024]{2,1,0:T(8,128)(2,1)} %get-tuple-element.223, s32[]{:T(128)} %get-tuple-element.210, bf16[1,4096,1024]{2,1,0:T(8,128)(2,1)} %all-gather.13.cloned.1.call-done, bf16[4,512,1024]{2,1,0:T(8,128)(2,1)} %get-tuple-element.225, ...), kind=kOutput, calls=%fused_computation.27.clone.1 | convolution fusion | flops 8634499072 | bytes 31458816 | tf_op jit(solution)/shard_map/while/body/eval_jaxpr/td,tf->df/dot_general | solution.py:43
  223.1 14.8 %fusion.67 = f32[4096,1024]{1,0:T(8,128)} fusion(bf16[512,4096]{1,0:T(8,128)(2,1)} %fusion.65, bf16[4,512,1024]{2,1,0:T(8,128)(2,1)} %get-tuple-element.225, s32[]{:T(128)} %get-tuple-element.210, pred[512]{0:T(512)(128)(4,1)S(1)} %dynamic-slice_reduce_fusion.2), kind=kOutput, calls=%fused_computation.22.clone.1 | convolution fusion | flops 4316463104 | bytes 22021120 | tf_op jit(solution)/shard_map/while/body/eval_jaxpr/tf,td->fd/dot_general | solution.py:42
  237.9 13.9 %reduce-scatter.3.cloned.1.call-done = f32[512,4096]{1,0:T(8,128)} async-done(((f32[1024,4096]{1,0:T(8,128)}), f32[512,4096]{1,0:T(8,128)}) %reduce-scatter.3.cloned.1.call-update) | async-done | bytes 8388624 | tf_op jit(solution)/shard_map/while/body/eval_jaxpr/reduce_scatter | solution.py:47
  251.8 11.6 %select_add_fusion.4 = f32[512,4096]{1,0:T(8,128)} fusion(f32[512,4096]{1,0:T(8,128)} %reduce-scatter.3.cloned.1.call-done, f32[512,4096]{1,0:T(8,128)} %get-tuple-element.211, pred[]{:T(512)S(6)} %compare.3), kind=kLoop, calls=%fused_computation.20.clone.1 | loop fusion | flops 4194304 | bytes 25165824 | tf_op jit(solution)/shard_map/while/body/eval_jaxpr/add | solution.py:47
  263.4 19.5 %reduce-scatter.5.cloned.1.call-done = f32[2048,1024]{1,0:T(8,128)} async-done(((f32[4096,1024]{1,0:T(8,128)}), f32[2048,1024]{1,0:T(8,128)}) %reduce-scatter.5.cloned.1.call-update) | async-done | bytes 8388624 | tf_op jit(solution)/shard_map/while/body/eval_jaxpr/reduce_scatter | solution.py:48
  282.8 12.2 %select_add_fusion.5 = f32[2048,1024]{1,0:T(8,128)} fusion(f32[2048,1024]{1,0:T(8,128)} %reduce-scatter.5.cloned.1.call-done, f32[2048,1024]{1,0:T(8,128)} %get-tuple-element.212, pred[]{:T(512)S(6)} %compare.3), kind=kLoop, calls=%fused_computation.19.clone.1 | loop fusion | flops 4194304 | bytes 25165824 | tf_op jit(solution)/shard_map/while/body/eval_jaxpr/add | solution.py:48
  296.4 25.9 %all-gather.11.cloned.1.call-done = bf16[1,1024,4096]{2,1,0:T(8,128)(2,1)} async-done(((bf16[1,512,4096]{2,1,0:T(8,128)(2,1)}), bf16[1,1024,4096]{2,1,0:T(8,128)(2,1)}) %all-gather.11.cloned.1.call-update) | async-done | bytes 8388624 | tf_op jit(solution)/shard_map/while/body/eval_jaxpr/all_gather | solution.py:8
  332.5 16.2 %all-gather.13.cloned.1.call-done = bf16[1,4096,1024]{2,1,0:T(8,128)(2,1)} async-done(((bf16[1,2048,1024]{2,1,0:T(8,128)(2,1)}), bf16[1,4096,1024]{2,1,0:T(8,128)(2,1)}) %all-gather.13.cloned.1.call-update) | async-done | bytes 8388624 | tf_op jit(solution)/shard_map/while/body/eval_jaxpr/all_gather | solution.py:8
  348.7 18.2 %fusion.66 = f32[1024,4096]{1,0:T(8,128)} fusion(bf16[512,4096]{1,0:T(8,128)(2,1)} %fusion.65, bf16[4,512,1024]{2,1,0:T(8,128)(2,1)} %get-tuple-element.223, s32[]{:T(128)} %get-tuple-element.210, bf16[1,4096,1024]{2,1,0:T(8,128)(2,1)} %all-gather.13.cloned.1.call-done, bf16[4,512,1024]{2,1,0:T(8,128)(2,1)} %get-tuple-element.225, ...), kind=kOutput, calls=%fused_computation.27.clone.1 | convolution fusion | flops 8634499072 | bytes 31458816 | tf_op jit(solution)/shard_map/while/body/eval_jaxpr/td,tf->df/dot_general | solution.py:43
  367.0 14.8 %fusion.67 = f32[4096,1024]{1,0:T(8,128)} fusion(bf16[512,4096]{1,0:T(8,128)(2,1)} %fusion.65, bf16[4,512,1024]{2,1,0:T(8,128)(2,1)} %get-tuple-element.225, s32[]{:T(128)} %get-tuple-element.210, pred[512]{0:T(512)(128)(4,1)S(1)} %dynamic-slice_reduce_fusion.2), kind=kOutput, calls=%fused_computation.22.clone.1 | convolution fusion | flops 4316463104 | bytes 22021120 | tf_op jit(solution)/shard_map/while/body/eval_jaxpr/tf,td->fd/dot_general | solution.py:42
  381.8 13.9 %reduce-scatter.3.cloned.1.call-done = f32[512,4096]{1,0:T(8,128)} async-done(((f32[1024,4096]{1,0:T(8,128)}), f32[512,4096]{1,0:T(8,128)}) %reduce-scatter.3.cloned.1.call-update) | async-done | bytes 8388624 | tf_op jit(solution)/shard_map/while/body/eval_jaxpr/reduce_scatter | solution.py:47
  395.7 11.6 %select_add_fusion.4 = f32[512,4096]{1,0:T(8,128)} fusion(f32[512,4096]{1,0:T(8,128)} %reduce-scatter.3.cloned.1.call-done, f32[512,4096]{1,0:T(8,128)} %get-tuple-element.211, pred[]{:T(512)S(6)} %compare.3), kind=kLoop, calls=%fused_computation.20.clone.1 | loop fusion | flops 4194304 | bytes 25165824 | tf_op jit(solution)/shard_map/while/body/eval_jaxpr/add | solution.py:47
  407.2 19.3 %reduce-scatter.5.cloned.1.call-done = f32[2048,1024]{1,0:T(8,128)} async-done(((f32[4096,1024]{1,0:T(8,128)}), f32[2048,1024]{1,0:T(8,128)}) %reduce-scatter.5.cloned.1.call-update) | async-done | bytes 8388624 | tf_op jit(solution)/shard_map/while/body/eval_jaxpr/reduce_scatter | solution.py:48
  426.5 12.2 %select_add_fusion.5 = f32[2048,1024]{1,0:T(8,128)} fusion(f32[2048,1024]{1,0:T(8,128)} %reduce-scatter.5.cloned.1.call-done, f32[2048,1024]{1,0:T(8,128)} %get-tuple-element.212, pred[]{:T(512)S(6)} %compare.3), kind=kLoop, calls=%fused_computation.19.clone.1 | loop fusion | flops 4194304 | bytes 25165824 | tf_op jit(solution)/shard_map/while/body/eval_jaxpr/add | solution.py:48
  440.1 25.9 %all-gather.11.cloned.1.call-done = bf16[1,1024,4096]{2,1,0:T(8,128)(2,1)} async-done(((bf16[1,512,4096]{2,1,0:T(8,128)(2,1)}), bf16[1,1024,4096]{2,1,0:T(8,128)(2,1)}) %all-gather.11.cloned.1.call-update) | async-done | bytes 8388624 | tf_op jit(solution)/shard_map/while/body/eval_jaxpr/all_gather | solution.py:8
  476.2 16.2 %all-gather.13.cloned.1.call-done = bf16[1,4096,1024]{2,1,0:T(8,128)(2,1)} async-done(((bf16[1,2048,1024]{2,1,0:T(8,128)(2,1)}), bf16[1,4096,1024]{2,1,0:T(8,128)(2,1)}) %all-gather.13.cloned.1.call-update) | async-done | bytes 8388624 | tf_op jit(solution)/shard_map/while/body/eval_jaxpr/all_gather | solution.py:8
  492.5 18.2 %fusion.66 = f32[1024,4096]{1,0:T(8,128)} fusion(bf16[512,4096]{1,0:T(8,128)(2,1)} %fusion.65, bf16[4,512,1024]{2,1,0:T(8,128)(2,1)} %get-tuple-element.223, s32[]{:T(128)} %get-tuple-element.210, bf16[1,4096,1024]{2,1,0:T(8,128)(2,1)} %all-gather.13.cloned.1.call-done, bf16[4,512,1024]{2,1,0:T(8,128)(2,1)} %get-tuple-element.225, ...), kind=kOutput, calls=%fused_computation.27.clone.1 | convolution fusion | flops 8634499072 | bytes 31458816 | tf_op jit(solution)/shard_map/while/body/eval_jaxpr/td,tf->df/dot_general | solution.py:43
  510.7 14.8 %fusion.67 = f32[4096,1024]{1,0:T(8,128)} fusion(bf16[512,4096]{1,0:T(8,128)(2,1)} %fusion.65, bf16[4,512,1024]{2,1,0:T(8,128)(2,1)} %get-tuple-element.225, s32[]{:T(128)} %get-tuple-element.210, pred[512]{0:T(512)(128)(4,1)S(1)} %dynamic-slice_reduce_fusion.2), kind=kOutput, calls=%fused_computation.22.clone.1 | convolution fusion | flops 4316463104 | bytes 22021120 | tf_op jit(solution)/shard_map/while/body/eval_jaxpr/tf,td->fd/dot_general | solution.py:42
  525.5 13.9 %reduce-scatter.3.cloned.1.call-done = f32[512,4096]{1,0:T(8,128)} async-done(((f32[1024,4096]{1,0:T(8,128)}), f32[512,4096]{1,0:T(8,128)}) %reduce-scatter.3.cloned.1.call-update) | async-done | bytes 8388624 | tf_op jit(solution)/shard_map/while/body/eval_jaxpr/reduce_scatter | solution.py:47
  539.4 11.6 %select_add_fusion.4 = f32[512,4096]{1,0:T(8,128)} fusion(f32[512,4096]{1,0:T(8,128)} %reduce-scatter.3.cloned.1.call-done, f32[512,4096]{1,0:T(8,128)} %get-tuple-element.211, pred[]{:T(512)S(6)} %compare.3), kind=kLoop, calls=%fused_computation.20.clone.1 | loop fusion | flops 4194304 | bytes 25165824 | tf_op jit(solution)/shard_map/while/body/eval_jaxpr/add | solution.py:47
  551.0 19.3 %reduce-scatter.5.cloned.1.call-done = f32[2048,1024]{1,0:T(8,128)} async-done(((f32[4096,1024]{1,0:T(8,128)}), f32[2048,1024]{1,0:T(8,128)}) %reduce-scatter.5.cloned.1.call-update) | async-done | bytes 8388624 | tf_op jit(solution)/shard_map/while/body/eval_jaxpr/reduce_scatter | solution.py:48
  570.3 12.2 %select_add_fusion.5 = f32[2048,1024]{1,0:T(8,128)} fusion(f32[2048,1024]{1,0:T(8,128)} %reduce-scatter.5.cloned.1.call-done, f32[2048,1024]{1,0:T(8,128)} %get-tuple-element.212, pred[]{:T(512)S(6)} %compare.3), kind=kLoop, calls=%fused_computation.19.clone.1 | loop fusion | flops 4194304 | bytes 25165824 | tf_op jit(solution)/shard_map/while/body/eval_jaxpr/add | solution.py:48
  583.1 222.2 %all-reduce.3.cloned.1.call-done = (f32[1,512,4096]{2,1,0:T(8,128)}, f32[1,2048,1024]{2,1,0:T(8,128)}) async-done(((f32[1,512,4096]{2,1,0:T(8,128)}, f32[1,2048,1024]{2,1,0:T(8,128)}), (f32[1,512,4096]{2,1,0:T(8,128)}, f32[1,2048,1024]{2,1,0:T(8,128)})) %all-reduce.3.cloned.1.call-update) | async-done | bytes 16777232 | tf_op jit(solution)/shard_map/psum | solution.py:54
  (51 shorter events, 78.0 us)
Async XLA Ops:
  8.7 28.5 %all-gather.11.cloned.1.call-start = ((), (), s32[]{:S(2)}) async-start(), calls=%async_computation.3 | async-start | bytes 12582912 | tf_op jit(solution)/shard_map/while/body/eval_jaxpr/all_gather | solution.py:8
  9.5 54.3 %all-gather.13.cloned.1.call-start = ((), (), s32[]{:S(2)}) async-start(), calls=%async_computation.4 | async-start | bytes 12582912 | tf_op jit(solution)/shard_map/while/body/eval_jaxpr/all_gather | solution.py:8
  10.2 100.5 %reduce-scatter.3.cloned.1.call-start = ((), (), s32[]{:S(2)}) async-start(), calls=%async_computation.5 | async-start | bytes 25165824 | tf_op jit(solution)/shard_map/while/body/eval_jaxpr/reduce_scatter | solution.py:47
  82.0 59.6 %reduce-scatter.5.cloned.1.call-start = ((), (), s32[]{:S(2)}) async-start(), calls=%async_computation.6 | async-start | bytes 25165824 | tf_op jit(solution)/shard_map/while/body/eval_jaxpr/reduce_scatter | solution.py:48
  151.4 27.1 %all-gather.11.cloned.1.call-start = ((), (), s32[]{:S(2)}) async-start(), calls=%async_computation.3 | async-start | bytes 12582912 | tf_op jit(solution)/shard_map/while/body/eval_jaxpr/all_gather | solution.py:8
  152.0 52.9 %all-gather.13.cloned.1.call-start = ((), (), s32[]{:S(2)}) async-start(), calls=%async_computation.4 | async-start | bytes 12582912 | tf_op jit(solution)/shard_map/while/body/eval_jaxpr/all_gather | solution.py:8
  152.5 99.2 %reduce-scatter.3.cloned.1.call-start = ((), (), s32[]{:S(2)}) async-start(), calls=%async_computation.5 | async-start | bytes 25165824 | tf_op jit(solution)/shard_map/while/body/eval_jaxpr/reduce_scatter | solution.py:47
  223.0 59.8 %reduce-scatter.5.cloned.1.call-start = ((), (), s32[]{:S(2)}) async-start(), calls=%async_computation.6 | async-start | bytes 25165824 | tf_op jit(solution)/shard_map/while/body/eval_jaxpr/reduce_scatter | solution.py:48
  295.0 27.3 %all-gather.11.cloned.1.call-start = ((), (), s32[]{:S(2)}) async-start(), calls=%async_computation.3 | async-start | bytes 12582912 | tf_op jit(solution)/shard_map/while/body/eval_jaxpr/all_gather | solution.py:8
  295.7 53.0 %all-gather.13.cloned.1.call-start = ((), (), s32[]{:S(2)}) async-start(), calls=%async_computation.4 | async-start | bytes 12582912 | tf_op jit(solution)/shard_map/while/body/eval_jaxpr/all_gather | solution.py:8
  296.3 99.3 %reduce-scatter.3.cloned.1.call-start = ((), (), s32[]{:S(2)}) async-start(), calls=%async_computation.5 | async-start | bytes 25165824 | tf_op jit(solution)/shard_map/while/body/eval_jaxpr/reduce_scatter | solution.py:47
  367.0 59.6 %reduce-scatter.5.cloned.1.call-start = ((), (), s32[]{:S(2)}) async-start(), calls=%async_computation.6 | async-start | bytes 25165824 | tf_op jit(solution)/shard_map/while/body/eval_jaxpr/reduce_scatter | solution.py:48
  438.8 27.3 %all-gather.11.cloned.1.call-start = ((), (), s32[]{:S(2)}) async-start(), calls=%async_computation.3 | async-start | bytes 12582912 | tf_op jit(solution)/shard_map/while/body/eval_jaxpr/all_gather | solution.py:8
  439.5 53.0 %all-gather.13.cloned.1.call-start = ((), (), s32[]{:S(2)}) async-start(), calls=%async_computation.4 | async-start | bytes 12582912 | tf_op jit(solution)/shard_map/while/body/eval_jaxpr/all_gather | solution.py:8
  440.1 99.3 %reduce-scatter.3.cloned.1.call-start = ((), (), s32[]{:S(2)}) async-start(), calls=%async_computation.5 | async-start | bytes 25165824 | tf_op jit(solution)/shard_map/while/body/eval_jaxpr/reduce_scatter | solution.py:47
  510.7 59.6 %reduce-scatter.5.cloned.1.call-start = ((), (), s32[]{:S(2)}) async-start(), calls=%async_computation.6 | async-start | bytes 25165824 | tf_op jit(solution)/shard_map/while/body/eval_jaxpr/reduce_scatter | solution.py:48
  582.5 222.8 %all-reduce.3.cloned.1.call-start = ((), (), s32[]{:S(2)}) async-start(), calls=%async_computation.2 | async-start | bytes 33554432 | tf_op jit(solution)/shard_map/psum | solution.py:54
  805.3 7.9 copy-start
Sparse Core Ops, SparseCore 0:
  11.2 25.9 all-gather.10
  38.9 24.8 all-gather.12
  82.1 28.5 reduce-scatter.2
  112.9 28.5 reduce-scatter.4
  153.5 24.8 all-gather.10
  179.9 24.8 all-gather.12
  223.2 28.5 reduce-scatter.2
  254.2 28.5 reduce-scatter.4
  297.5 24.8 all-gather.10
  323.8 24.8 all-gather.12
  367.1 28.5 reduce-scatter.2
  397.9 28.5 reduce-scatter.4
  441.2 24.8 all-gather.10
  467.6 24.8 all-gather.12
  510.8 28.5 reduce-scatter.2
  541.7 28.5 reduce-scatter.4
Sparse Core Ops, SparseCore 1:
  589.3 215.9 all-reduce.2
where the time goes:
time: 824 us
  waiting for transfers between devices  533 us (65%)
  matrix products  172 us (21%)
  other arithmetic  91 us (11%)
  between operations  15.2 us (2%)
  local copies, waits for them, and re-layouts  11.4 us (1%)
    psum x1, waiting for transfers between devices, device_grads(): grad_up = lax.psum(jnp.stack(acc_up), 'replica')  222 us
    all_gather x8, waiting for transfers between devices, gather_full(): return lax.all_gather(w_shard, 'fsdp', axis=0, tiled=True)  170 us
    reduce_scatter x4, waiting for transfers between devices, micro_step(): lax.psum_scatter(gw_down, 'fsdp', scatter_dimension=0, tiled=True)  79.8 us
    dot_general x4, matrix products, micro_step(): jnp.einsum('td,tf->df', x_prev, grad_hid, preferred_element_type=jnp.floa...  72.8 us
    dot_general x4, matrix products, micro_step(): jnp.einsum('tf,td->fd', act_bf, grad_x, preferred_element_type=jnp.float32)  59 us
    reduce_scatter x4, waiting for transfers between devices, micro_step(): lax.psum_scatter(gw_up, 'fsdp', scatter_dimension=0, tiled=True)  55.5 us
    add x4, other arithmetic, micro_step(): new_down[layer_idx]  46.4 us
    add x4, other arithmetic, micro_step(): new_up[layer_idx]  43.9 us
  transfers between devices with their start and end apart: 17, of which 17 were waited for; matrix products, arithmetic and copies ran while one was open for 17% of the time, Pallas kernels for 0%

commit v1 on v0

v1 whole, which is shorter than its diff:
```python
import jax
import jax.numpy as jnp
from jax import lax
from jax.sharding import PartitionSpec as P


def solution(mesh):
    tok_spec = P(None, ("model", "replica", "fsdp"), None)
    len_spec = P(None, ("model", "replica", "fsdp"))
    w_spec = P(None, ("model", "fsdp"), None)

    def device_grads(x_in, dy_out, lengths, w_up, w_down):
        n_micro, tok_dev, d_model = x_in.shape
        mask = jnp.arange(tok_dev)[None, :] < lengths
        up_full = lax.all_gather(w_up[0], "fsdp", axis=0, tiled=True)
        down_full = lax.all_gather(w_down[0], "fsdp", axis=0, tiled=True)
        x = x_in.reshape(n_micro * tok_dev, d_model)
        dy = jnp.where(mask[:, :, None], dy_out, jnp.zeros_like(dy_out)).reshape(n_micro * tok_dev, d_model)
        hidden = jnp.dot(x, up_full, preferred_element_type=jnp.float32).astype(jnp.bfloat16)
        act_f32, gelu_vjp = jax.vjp(jax.nn.gelu, hidden.astype(jnp.float32))
        act_bf = act_f32.astype(jnp.bfloat16)
        grad_act = jnp.einsum("td,fd->tf", dy, down_full, preferred_element_type=jnp.float32)
        grad_hid = gelu_vjp(grad_act)[0].astype(jnp.bfloat16)
        gw_down = jnp.einsum("tf,td->fd", act_bf, dy, preferred_element_type=jnp.float32)
        gw_up = jnp.einsum("td,tf->df", x, grad_hid, preferred_element_type=jnp.float32)
        grad_down = lax.psum(lax.psum_scatter(gw_down, "fsdp", scatter_dimension=0, tiled=True), "replica")
        grad_up = lax.psum(lax.psum_scatter(gw_up, "fsdp", scatter_dimension=0, tiled=True), "replica")
        return grad_up[None], grad_down[None]

    return jax.shard_map(device_grads, mesh=mesh, in_specs=(tok_spec, tok_spec, len_spec, w_spec, w_spec), out_specs=(w_spec, w_spec), check_vma=False)
```

time: 824 us -> 435 us (0.53)
  waiting for transfers between devices: 533 us -> 279 us
  other arithmetic: 91 us -> 4.55 us
  matrix products: 172 us -> 120 us
    all_gather x8 -> x2, waiting for transfers between devices: 170 us -> 24.7 us  [the longest x1 22.4 us: device_grads(): up_full = lax.all_gather(w_up[0], 'fsdp', axis=0, tiled=True)]
    reduce_scatter x8 -> x2, waiting for transfers between devices: 135 us -> 30.6 us  [the longest x1 30.6 us: device_grads(): lax.psum_scatter(gw_down, 'fsdp', scatter_dimension=0, tiled=True)]
    add x8 -> x0, other arithmetic: 90.3 us -> none  [the longest x4 46.4 us: micro_step(): new_down[layer_idx]]
    dot_general x12 -> x4, matrix products: 172 us -> 120 us  [the longest x1 44.4 us: device_grads(): jnp.einsum('td,fd->tf', dy, down_full, preferred_element_type=jnp.float32)]
  transfers between devices with their start and end apart: 17 -> 5, of which waited for: 17 -> 4; matrix products, arithmetic and copies ran while one was open for 17% -> 13% of each run, Pallas kernels for 0% -> 0%
where the time goes in v1:
time: 435 us
  waiting for transfers between devices  279 us (64%)
  matrix products  120 us (28%)
  local copies, waits for them, and re-layouts  17.3 us (4%)
  between operations  13.8 us (3%)
  other arithmetic  4.55 us (1%)
    psum x1, waiting for transfers between devices, device_grads(): lax.psum(lax.psum_scatter(gw_up, 'fsdp', scatter_dimension=0, tiled=True)...  222 us
    dot_general x1, matrix products, device_grads(): jnp.einsum('td,fd->tf', dy, down_full, preferred_element_type=jnp.float32)  44.4 us
    reduce_scatter x1, waiting for transfers between devices, device_grads(): lax.psum_scatter(gw_down, 'fsdp', scatter_dimension=0, tiled=True)  30.6 us
    dot_general x1, matrix products, device_grads(): jnp.einsum('tf,td->fd', act_bf, dy, preferred_element_type=jnp.float32)  28.9 us
    dot_general x1, matrix products, device_grads(): jnp.dot(x, up_full, preferred_element_type=jnp.float32).astype(jnp.bfloat16)  24.2 us
    dot_general x1, matrix products, device_grads(): jnp.einsum('td,tf->df', x, grad_hid, preferred_element_type=jnp.float32)  22.9 us
    all_gather x1, waiting for transfers between devices, device_grads(): up_full = lax.all_gather(w_up[0], 'fsdp', axis=0, tiled=True)  22.4 us
    unnamed x4, local copies, waits for them, and re-layouts  17.3 us
  transfers between devices with their start and end apart: 5, of which 4 were waited for; matrix products, arithmetic and copies ran while one was open for 13% of the time, Pallas kernels for 0%

profile of v1, /device:TPU:0, one launch (start us, length us, event | category | flops | bytes accessed | tf_op | source)
XLA Modules:
  0.0 434.8 jit_solution(5600141925063260529)
XLA Ops:
  7.2 0.0 all-gather.7.cloned.1.call-start
  7.2 0.7 all-gather.7.cloned.1.call-update
  7.9 0.0 all-gather.5.cloned.1.call-start
  7.9 0.7 all-gather.5.cloned.1.call-update
  8.6 0.0 reduce-scatter.3.cloned.1.call-start
  8.7 0.7 iota_compare_fusion
  9.4 3.8 broadcast_select_fusion
  13.2 22.4 %all-gather.7.cloned.1.call-done = bf16[1,1024,4096]{2,1,0:T(8,128)(2,1)} async-done(((bf16[1,512,4096]{2,1,0:T(8,128)(2,1)}), bf16[1,1024,4096]{2,1,0:T(8,128)(2,1)}) %all-gather.7.cloned.1.call-update) | async-done | bytes 8388624 | tf_op jit(solution)/shard_map/all_gather | solution.py:15
  35.7 24.2 %convolution_convert_fusion = bf16[2048,4096]{1,0:T(8,128)(2,1)} fusion(bf16[2048,1024]{1,0:T(8,128)(2,1)} %bitcast.35, bf16[1,1024,4096]{2,1,0:T(8,128)(2,1)} %all-gather.7.cloned.1.call-done), kind=kOutput, calls=%fused_computation.17 | convolution fusion | flops 17188257792 | bytes 29360128 | tf_op jit(solution)/shard_map/dot_general | solution.py:19
  59.9 2.3 all-gather.5.cloned.1.call-done
  62.2 0.0 copy-start
  62.2 44.4 %fusion.47 = bf16[2048,4096]{1,0:T(8,128)(2,1)} fusion(bf16[2048,4096]{1,0:T(8,128)(2,1)} %convolution_convert_fusion, bf16[2048,1024]{1,0:T(8,128)(2,1)} %bitcast.32, bf16[1,4096,1024]{2,1,0:T(8,128)(2,1)} %all-gather.5.cloned.1.call-done), kind=kOutput, calls=%fused_computation.8.clone.clone.clone.clone.1 | convolution fusion | flops 17356029952 | bytes 46137344 | tf_op jit(solution)/shard_map/td,fd->tf/dot_general | solution.py:22
  106.6 0.0 copy-done
  106.6 22.9 %fusion.14 = f32[1024,4096]{0,1:T(8,128)} fusion(bf16[2048,1024]{1,0:T(8,128)(2,1)S(1)} %bitcast.36, bf16[2048,4096]{1,0:T(8,128)(2,1)} %fusion.47), kind=kOutput, calls=%fused_computation.18 | convolution fusion | flops 17179869184 | bytes 37748736 | tf_op jit(solution)/shard_map/td,tf->df/dot_general | solution.py:25
  129.5 0.0 reduce-scatter.3.cloned.1.call-update
  129.5 0.0 reduce-scatter.5.cloned.1.call-start
  129.6 28.9 %fusion.10 = f32[4096,1024]{1,0:T(8,128)} fusion(bf16[2048,1024]{1,0:T(8,128)(2,1)} %bitcast.33, bf16[2048,4096]{1,0:T(8,128)(2,1)} %convolution_convert_fusion), kind=kOutput, calls=%fused_computation.15 | convolution fusion | flops 17263755264 | bytes 37748736 | tf_op jit(solution)/shard_map/tf,td->fd/dot_general | solution.py:24
  158.4 0.0 reduce-scatter.5.cloned.1.call-update
  158.5 0.0 all-reduce.3.cloned.1.call-start
  158.5 0.0 reduce-scatter.3.cloned.1.call-done
  158.5 30.6 %reduce-scatter.5.cloned.1.call-done = f32[2048,1024]{1,0:T(8,128)} async-done(((f32[4096,1024]{1,0:T(8,128)}), f32[2048,1024]{1,0:T(8,128)}) %reduce-scatter.5.cloned.1.call-update) | async-done | bytes 8388624 | tf_op jit(solution)/shard_map/reduce_scatter | solution.py:26
  189.2 0.0 all-reduce.3.cloned.1.call-update
  189.2 221.7 %all-reduce.3.cloned.1.call-done = (f32[1,512,4096]{1,2,0:T(8,128)}, f32[1,2048,1024]{2,1,0:T(8,128)}) async-done(((f32[1,512,4096]{1,2,0:T(8,128)}, f32[1,2048,1024]{2,1,0:T(8,128)}), (f32[1,512,4096]{1,2,0:T(8,128)}, f32[1,2048,1024]{2,1,0:T(8,128)})) %all-reduce.3.cloned.1.call-update) | async-done | bytes 16777232 | tf_op jit(solution)/shard_map/psum | solution.py:27
  410.9 8.9 %copy.7 = f32[1,512,4096]{2,1,0:T(8,128)} copy(f32[1,512,4096]{1,2,0:T(8,128)} %get-tuple-element.4) | data formatting | bytes 16777216
  419.8 8.4 %copy.10 = f32[1,2048,1024]{2,1,0:T(8,128)} copy(f32[1,2048,1024]{2,1,0:T(8,128)} %get-tuple-element.7) | data formatting | bytes 16777216
Async XLA Ops:
  7.2 28.5 %all-gather.7.cloned.1.call-start = ((), (), s32[]{:S(2)}) async-start(), calls=%async_computation.5 | async-start | bytes 12582912 | tf_op jit(solution)/shard_map/all_gather | solution.py:15
  7.9 54.3 %all-gather.5.cloned.1.call-start = ((), (), s32[]{:S(2)}) async-start(), calls=%async_computation.4 | async-start | bytes 12582912 | tf_op jit(solution)/shard_map/all_gather | solution.py:16
  8.6 149.9 %reduce-scatter.3.cloned.1.call-start = ((), (), s32[]{:S(2)}) async-start(), calls=%async_computation.2 | async-start | bytes 25165824 | tf_op jit(solution)/shard_map/reduce_scatter | solution.py:27
  62.2 44.4 %copy-start = (bf16[4,512,1024]{2,1,0:T(8,128)(2,1)S(1)}, bf16[4,512,1024]{2,1,0:T(8,128)(2,1)}, u32[]{:S(2)}) copy-start(bf16[4,512,1024]{2,1,0:T(8,128)(2,1)} %param.5) | copy-start | bytes 12582916
  129.5 59.6 %reduce-scatter.5.cloned.1.call-start = ((), (), s32[]{:S(2)}) async-start(), calls=%async_computation.3 | async-start | bytes 25165824 | tf_op jit(solution)/shard_map/reduce_scatter | solution.py:26
  158.5 252.4 %all-reduce.3.cloned.1.call-start = ((), (), s32[]{:S(2)}) async-start(), calls=%async_computation.6 | async-start | bytes 33554432 | tf_op jit(solution)/shard_map/psum | solution.py:27
Sparse Core Ops, SparseCore 0:
  9.6 25.9 all-gather.6
  37.3 24.8 all-gather.4
  129.6 28.6 reduce-scatter.2
  160.5 28.5 reduce-scatter.4
  194.8 216.0 all-reduce.2

commit v2 on v1

v2 whole, which is shorter than its diff:
```python
import functools

import jax
import jax.numpy as jnp
from jax import lax
from jax.experimental import pallas as pl
from jax.experimental.pallas import tpu as pltpu
from jax.sharding import PartitionSpec as P

F32, BF16 = jnp.float32, jnp.bfloat16
MESH_ID = pl.DeviceIdType.MESH
SQRT_2_OVER_PI = 0.7978845608028654
CUBIC = 0.044715
NT_DIMS = (((1,), (1,)), ((), ()))

FC = 256
RING = 4
ROWS = 512
PH_ROWS = (128, 32, 8)
PH_OFF = (0, 384, 480)
R_ROWS = 504
W_SLOTS = 3
P_SLOTS = 2

SCHEDULE = (
    ("pair", 1),
    ("rs0b", 3),
    ("rs0c", 5),
    ("rs1b", 7),
    ("rs1c", 9),
    ("rs2b", 11),
    ("rs2c", 13),
    ("ag2b", 15),
    ("ag2c", 17),
    ("ag1b", 19),
    ("ag1c", 21),
    ("ag0b", 23),
    ("ag0c", 25),
    ("done", 29),
)


def gelu_and_slope(u):
    u2 = u * u
    t = jnp.tanh(SQRT_2_OVER_PI * (u + CUBIC * (u2 * u)))
    half = 0.5 * (1.0 + t)
    slope = half + 0.5 * u * (1.0 - t * t) * (SQRT_2_OVER_PI + (3.0 * CUBIC * SQRT_2_OVER_PI) * u2)
    return u * half, slope


def kernel(n_ticks, n_tok, n_micro,
           x_hbm, dy_hbm, len_ref, wu_hbm, wd_hbm, gu_hbm, gd_hbm,
           X, DY, XT, WU, WD, AT, DH, SU, SD, RU, RD, G, R, E,
           in_sem, w_local, w_send, w_recv, p_send, p_recv, rs1, rs2, ag1, ag2, send0, out_send, out_sem,
           g_free, w_credit, ru_credit, rd_credit):
    n_items = 2 * n_ticks
    tok = n_tok // n_micro
    rep = lax.axis_index("replica")
    me = lax.axis_index("fsdp")
    mate = 1 - me

    def dev(replica, core):
        return (0, replica, core)

    def axis_of(item, phase):
        a = (item + phase) % 3
        stride = 1 + 3 * a + 9 * ((a * (a - 1)) // 2)
        c = (rep // stride) % RING
        return stride, c

    def neighbour(stride, c, d):
        return rep + stride * ((c + d + RING) % RING - c)

    def base_of(item, phase):
        b = 0
        for p in range(phase):
            b = b + axis_of(item, p)[1] * PH_ROWS[p]
        return b

    def g_rows(item, h, start, n):
        row = pl.multiple_of(item * (2 * ROWS) + h * ROWS + start, 8)
        return G.at[pl.ds(row, n)]

    def r_rows(item, h, start, n):
        row = pl.multiple_of(item * (2 * R_ROWS) + h * R_ROWS + start, 8)
        return R.at[pl.ds(row, n)]

    def e_rows(item, h, start, n):
        row = pl.multiple_of(item * (2 * PH_ROWS[0]) + h * PH_ROWS[0] + start, 8)
        return E.at[pl.ds(row, n)]

    def wait_rows(sem, n):
        ref = G.at[pl.ds(0, n)]
        pltpu.make_async_copy(ref, ref, sem).wait()

    barrier = pltpu.get_barrier_semaphore()
    for a in range(3):
        stride = RING**a
        c = (rep // stride) % RING
        for d in (1, -1):
            pl.semaphore_signal(barrier, inc=1, device_id=dev(neighbour(stride, c, d), me), device_id_type=MESH_ID)
    pl.semaphore_signal(barrier, inc=1, device_id=dev(rep, mate), device_id_type=MESH_ID)

    def x_copy(k):
        return pltpu.make_async_copy(x_hbm.at[k], X.at[pl.ds(k * tok, tok)], in_sem.at[k])

    def dy_copy(k):
        return pltpu.make_async_copy(dy_hbm.at[k], DY.at[pl.ds(k * tok, tok)], in_sem.at[n_micro + k])

    for k in range(n_micro):
        x_copy(k).start()
    for k in range(n_micro):
        dy_copy(k).start()

    def w_copies(t):
        slot = t % W_SLOTS
        lo = pl.multiple_of(t * 128, 128)
        hi = pl.multiple_of(n_ticks * 128 + t * 128, 128)
        up_rows = pl.ds(pl.multiple_of(me * 512, 512), 512)
        down_rows = pl.ds(pl.multiple_of(me * 128, 128), 128)
        pairs = (
            (wu_hbm.at[0, :, pl.ds(lo, 128)], WU.at[slot, up_rows, pl.ds(0, 128)]),
            (wu_hbm.at[0, :, pl.ds(hi, 128)], WU.at[slot, up_rows, pl.ds(128, 128)]),
            (wd_hbm.at[0, pl.ds(lo, 128), :], WD.at[slot, down_rows, :]),
        )
        local = [pltpu.make_async_copy(s, d, w_local.at[slot]) for s, d in pairs]
        remote = [
            pltpu.make_async_remote_copy(s, d, w_send.at[slot], w_recv.at[slot], device_id=dev(rep, mate), device_id_type=MESH_ID)
            for s, d in pairs
        ]
        return local, remote

    def start_w(t):
        local, remote = w_copies(t)
        for c in local + remote:
            c.start()

    def wait_w(t):
        slot = t % W_SLOTS
        ref = WU.at[slot]
        for sem in (w_local, w_recv, w_send):
            pltpu.make_async_copy(ref, ref, sem.at[slot]).wait()

    pl.semaphore_wait(barrier, 7)
    start_w(0)
    if n_ticks > 1:
        start_w(1)

    rb = min(256, tok)
    for k in range(n_micro):
        x_copy(k).wait()

        def transpose_rows(s, carry, k=k):
            rows = pl.ds(pl.multiple_of(k * tok + s * rb, rb), rb)
            XT[:, rows] = X[rows, :].T
            return carry

        lax.fori_loop(0, tok // rb, transpose_rows, 0)
    mb = min(64, tok)
    for k in range(n_micro):
        dy_copy(k).wait()
        n_valid = len_ref[k, 0]

        def mask_rows(s, carry, k=k, n_valid=n_valid):
            rows = pl.ds(pl.multiple_of(k * tok + s * mb, mb), mb)
            v = DY[rows, :].astype(F32)
            at = s * mb + lax.broadcasted_iota(jnp.int32, v.shape, 0)
            DY[rows, :] = jnp.where(at < n_valid, v, 0.0).astype(BF16)
            return carry

        lax.fori_loop(0, tok // mb, mask_rows, 0)

    cb = min(512, n_tok // 2)

    def hidden_block(t, half):
        slot = t % W_SLOTS
        if half == 0:
            wait_w(t)
        for s in range(n_tok // 2 // cb):
            rows = pl.ds(half * (n_tok // 2) + s * cb, cb)
            h = jnp.dot(X[rows, :], WU[slot], preferred_element_type=F32).astype(BF16).astype(F32)
            da = lax.dot_general(DY[rows, :], WD[slot], NT_DIMS, preferred_element_type=F32)
            a, slope = gelu_and_slope(h)
            AT[:, rows] = a.astype(BF16).T
            DH[rows, :] = (da * slope).astype(BF16)
        if half == 0:
            @pl.when(t + 2 < n_ticks)
            def _():
                @pl.when(t + 2 >= W_SLOTS)
                def _():
                    pl.semaphore_wait(w_credit, 1)
                start_w(t + 2)
        else:
            @pl.when(t + W_SLOTS < n_ticks)
            def _():
                pl.semaphore_signal(w_credit, inc=1, device_id=dev(rep, mate), device_id_type=MESH_ID)

    def pair_copy(t, up):
        slot = t % P_SLOTS
        if up:
            src, dst, item = SU.at[pl.ds(pl.multiple_of(mate * 512, 512), 512)], RU.at[slot], 2 * t
        else:
            src, dst, item = SD.at[pl.ds(pl.multiple_of(mate * 128, 128), 128)], RD.at[slot], 2 * t + 1
        return pltpu.make_async_remote_copy(
            src, dst, p_send.at[0 if up else 1], p_recv.at[item], device_id=dev(rep, mate), device_id_type=MESH_ID)

    def up_block(t):
        for s in range(2):
            rows = pl.ds(s * 512, 512)
            SU[rows, :] = jnp.dot(XT[rows, :], DH[...], preferred_element_type=F32)

        @pl.when(t >= P_SLOTS)
        def _():
            pl.semaphore_wait(ru_credit, 1)
        pair_copy(t, True).start()

    def down_block(t):
        for s in range(2):
            cols = pl.ds(s * 512, 512)
            SD[:, cols] = jnp.dot(AT[...], DY[:, cols], preferred_element_type=F32)

        @pl.when(t >= P_SLOTS)
        def _():
            pl.semaphore_wait(rd_credit, 1)
        pair_copy(t, False).start()

    def send(sent, src, dst, recv, to):
        pltpu.make_async_remote_copy(
            src, dst, sent, recv, device_id=dev(to, me), device_id_type=MESH_ID).start()

    def pair_stage(item, up):
        t = item // 2
        copy = pair_copy(t, up)
        copy.wait_recv()
        g0 = item * (2 * ROWS)
        slot = t % P_SLOTS
        if up:
            own = pl.ds(pl.multiple_of(me * 512, 512), 512)
            for h in range(2):
                cols = pl.ds(h * 128, 128)
                G[pl.ds(pl.multiple_of(g0 + h * ROWS, 8), ROWS), :] = SU[own, cols] + RU[slot, :, cols]
        else:
            own = pl.ds(pl.multiple_of(me * 128, 128), 128)
            for s in range(8):
                cols = pl.ds(s * 128, 128)
                G[pl.ds(pl.multiple_of(g0 + s * 128, 8), 128), :] = SD[own, cols] + RD[slot, :, cols]
        copy.wait_send()

        @pl.when(t + P_SLOTS < n_ticks)
        def _():
            pl.semaphore_signal(ru_credit if up else rd_credit, inc=1, device_id=dev(rep, mate), device_id_type=MESH_ID)
        rs_a(item, 0)

    def rs_a(item, p):
        stride, c = axis_of(item, p)
        m, off, b = PH_ROWS[p], PH_OFF[p], base_of(item, p)
        sent = (send0 if p == 0 else out_send).at[item]
        for h, d in ((0, 1), (1, -1)):
            send(sent, g_rows(item, h, b + (c + 2) % RING * m, m), r_rows(item, h, off, m), rs1.at[item * 3 + p], neighbour(stride, c, d))
        for h, d in ((0, 1), (1, -1)):
            send(sent, g_rows(item, h, b + (c - d + RING) % RING * m, m), r_rows(item, h, off + m, m), rs2.at[item * 3 + p], neighbour(stride, c, -d))

    def rs_b(item, p):
        stride, c = axis_of(item, p)
        m, off, b = PH_ROWS[p], PH_OFF[p], base_of(item, p)
        wait_rows(rs1.at[item * 3 + p], 2 * m)
        for h, d in ((0, 1), (1, -1)):
            g = g_rows(item, h, b + (c + d + RING) % RING * m, m)
            g[...] = g[...] + r_rows(item, h, off, m)[...]
            send((send0 if p == 0 else out_send).at[item], g, r_rows(item, h, off + 2 * m, m), rs2.at[item * 3 + p], neighbour(stride, c, d))

    def rs_c(item, p):
        stride, c = axis_of(item, p)
        m, off, b = PH_ROWS[p], PH_OFF[p], base_of(item, p)
        wait_rows(rs2.at[item * 3 + p], 4 * m)
        for h in range(2):
            g = g_rows(item, h, b + c * m, m)
            out = e_rows(item, h, b + c * m - base_of(item, 1), m) if p == 2 else g
            out[...] = g[...] + (r_rows(item, h, off + m, m)[...] + r_rows(item, h, off + 2 * m, m)[...])
        if p < 2:
            rs_a(item, p + 1)
        else:
            ag_a(item, 2)
        if p == 1:
            wait_rows(send0.at[item], 6 * PH_ROWS[0])
            stride, c = axis_of(item, 0)
            for d in (1, -1):
                pl.semaphore_signal(g_free.at[item], inc=1, device_id=dev(neighbour(stride, c, d), me), device_id_type=MESH_ID)

    def ag_part(item, h, p, q):
        m = PH_ROWS[p]
        if p == 0:
            return g_rows(item, h, q * m, m)
        return e_rows(item, h, base_of(item, p) - base_of(item, 1) + q * m, m)

    def ag_a(item, p):
        stride, c = axis_of(item, p)
        if p == 0:
            pl.semaphore_wait(g_free.at[item], 2)
        for recv, sign in ((ag1, 1), (ag2, -1)):
            for h, d in ((0, 1), (1, -1)):
                part = ag_part(item, h, p, c)
                src = e_rows(item, h, 0, PH_ROWS[0]) if p == 0 else part
                send(out_send.at[item], src, part, recv.at[item * 3 + p], neighbour(stride, c, sign * d))

    def ag_b(item, p):
        stride, c = axis_of(item, p)
        wait_rows(ag1.at[item * 3 + p], 2 * PH_ROWS[p])
        for h, d in ((0, 1), (1, -1)):
            part = ag_part(item, h, p, (c - d + RING) % RING)
            send(out_send.at[item], part, part, ag2.at[item * 3 + p], neighbour(stride, c, d))

    def out_copies(item, up):
        t = item // 2
        c = axis_of(item, 0)[1]
        lo = pl.multiple_of(t * 128, 128)
        hi = pl.multiple_of(n_ticks * 128 + t * 128, 128)
        copies = []
        for h in range(2):
            for k in range(RING):
                q = (c + k) % RING
                src = e_rows(item, h, 0, 128) if k == 0 else g_rows(item, h, q * 128, 128)
                if up:
                    dst = gu_hbm.at[0, pl.ds(pl.multiple_of(q * 128, 128), 128), pl.ds(hi if h else lo, 128)]
                else:
                    dst = gd_hbm.at[0, pl.ds(lo, 128), pl.ds(pl.multiple_of(h * 512 + q * 128, 128), 128)]
                copies.append(pltpu.make_async_copy(src, dst, out_sem.at[item]))
        return copies

    def ag_c(item, p, up):
        wait_rows(ag2.at[item * 3 + p], 4 * PH_ROWS[p])
        if p > 0:
            ag_a(item, p - 1)
        else:
            for copy in out_copies(item, up):
                copy.start()

    def finish(item):
        wait_rows(out_sem.at[item], 2 * ROWS)
        wait_rows(out_send.at[item], 4 * R_ROWS - 6 * PH_ROWS[0])

    def stage(name, item, up):
        if name == "pair":
            pair_stage(item, up)
        elif name == "done":
            finish(item)
        else:
            kind, p, part = name[:2], int(name[2]), name[3]
            if kind == "rs":
                (rs_b if part == "b" else rs_c)(item, p)
            elif part == "b":
                ag_b(item, p)
            else:
                ag_c(item, p, up)

    by_kind = ("pair", "ag0c")

    def step(u, carry):
        t = u // 4
        block = u % 4
        live = t < n_ticks
        pl.when(live & (block == 0))(lambda: hidden_block(t, 0))
        pl.when(live & (block == 1))(lambda: hidden_block(t, 1))
        pl.when(live & (block == 2))(lambda: up_block(t))
        pl.when(live & (block == 3))(lambda: down_block(t))
        for name, lag in SCHEDULE:
            v = u - lag + 4
            vt, vb = v // 4 - 1, v % 4
            item = 2 * vt + vb - 2
            inside = (vt >= 0) & (vt < n_ticks) & (vb >= 2)
            if name in by_kind:
                pl.when(inside & (vb == 2))(functools.partial(stage, name, item, True))
                pl.when(inside & (vb == 3))(functools.partial(stage, name, item, False))
            else:
                pl.when(inside)(functools.partial(stage, name, item, None))
        return carry

    lax.fori_loop(0, 4 * n_ticks + SCHEDULE[-1][1], step, 0)


def solution(mesh):
    tok_spec = P(None, ("model", "replica", "fsdp"), None)
    len_spec = P(None, ("model", "replica", "fsdp"))
    w_spec = P(None, ("model", "fsdp"), None)

    def device_grads(x_in, dy_out, lengths, w_up, w_down):
        n_micro, tok, d = x_in.shape
        n_tok = n_micro * tok
        d_ff = w_up.shape[2]
        n_ticks = d_ff // FC
        n_items = 2 * n_ticks
        any_spec = pl.BlockSpec(memory_space=pl.ANY)
        dma = pltpu.SemaphoreType.DMA
        return pl.pallas_call(
            functools.partial(kernel, n_ticks, n_tok, n_micro),
            out_shape=(
                jax.ShapeDtypeStruct(w_up.shape, F32),
                jax.ShapeDtypeStruct(w_down.shape, F32),
            ),
            in_specs=[any_spec, any_spec, pl.BlockSpec(memory_space=pltpu.SMEM), any_spec, any_spec],
            out_specs=(any_spec, any_spec),
            scratch_shapes=[
                pltpu.VMEM((n_tok, d), BF16),
                pltpu.VMEM((n_tok, d), BF16),
                pltpu.VMEM((d, n_tok), BF16),
                pltpu.VMEM((W_SLOTS, d, FC), BF16),
                pltpu.VMEM((W_SLOTS, FC, d), BF16),
                pltpu.VMEM((FC, n_tok), BF16),
                pltpu.VMEM((n_tok, FC), BF16),
                pltpu.VMEM((d, FC), F32),
                pltpu.VMEM((FC, d), F32),
                pltpu.VMEM((P_SLOTS, d // 2, FC), F32),
                pltpu.VMEM((P_SLOTS, FC // 2, d), F32),
                pltpu.VMEM((n_items * 2 * ROWS, 128), F32),
                pltpu.VMEM((n_items * 2 * R_ROWS, 128), F32),
                pltpu.VMEM((n_items * 2 * PH_ROWS[0], 128), F32),
                dma((2 * n_micro,)),
                dma((W_SLOTS,)),
                dma((W_SLOTS,)),
                dma((W_SLOTS,)),
                dma((2,)),
                dma((n_items,)),
                dma((3 * n_items,)),
                dma((3 * n_items,)),
                dma((3 * n_items,)),
                dma((3 * n_items,)),
                dma((n_items,)),
                dma((n_items,)),
                dma((n_items,)),
                pltpu.SemaphoreType.REGULAR((n_items,)),
                pltpu.SemaphoreType.REGULAR,
                pltpu.SemaphoreType.REGULAR,
                pltpu.SemaphoreType.REGULAR,
            ],
            compiler_params=pltpu.CompilerParams(
                collective_id=0, has_side_effects=True, vmem_limit_bytes=67043328),
            name="grads",
        )(x_in, dy_out, lengths, w_up, w_down)

    return jax.shard_map(device_grads, mesh=mesh, in_specs=(tok_spec, tok_spec, len_spec, w_spec, w_spec), out_specs=(w_spec, w_spec), check_vma=False)
```

time: 435 us -> 235 us (0.54)
  waiting for transfers between devices: 279 us -> 0 us
  Pallas kernels: 0 us -> 222 us
  matrix products: 120 us -> 0 us
  between operations: 13.8 us -> 0.65 us
  local copies, waits for them, and re-layouts: 17.3 us -> 12.6 us
  other arithmetic: 4.55 us -> 0 us
    pallas_call x0 -> x1, Pallas kernels: none -> 222 us  [device_grads(): pl.pallas_call(functools.partial(kernel, n_ticks, n_tok, n_micro), out_sh...]
    psum x1 -> x0, waiting for transfers between devices: 222 us -> none  [device_grads(): lax.psum(lax.psum_scatter(gw_up, 'fsdp', scatter_dimension=0, tiled=True)...]
    dot_general x4 -> x0, matrix products: 120 us -> none  [the longest x1 44.4 us: device_grads(): jnp.einsum('td,fd->tf', dy, down_full, preferred_element_type=jnp.float32)]
    reduce_scatter x2 -> x0, waiting for transfers between devices: 30.6 us -> none  [the longest x1 30.6 us: device_grads(): lax.psum_scatter(gw_down, 'fsdp', scatter_dimension=0, tiled=True)]
    all_gather x2 -> x0, waiting for transfers between devices: 24.7 us -> none  [the longest x1 22.4 us: device_grads(): up_full = lax.all_gather(w_up[0], 'fsdp', axis=0, tiled=True)]
    unnamed x4 -> x5, local copies, waits for them, and re-layouts: 17.3 us -> 12.6 us
  transfers between devices with their start and end apart: 5 -> 0, of which waited for: 4 -> 0; matrix products, arithmetic and copies ran while one was open for 13% -> 0% of each run, Pallas kernels for 0% -> 0%
where the time goes in v2:
time: 235 us
  Pallas kernels  222 us (94%)
  local copies, waits for them, and re-layouts  12.6 us (5%)
    pallas_call x1, Pallas kernels, device_grads(): pl.pallas_call(functools.partial(kernel, n_ticks, n_tok, n_micro), out_sh...  222 us
    unnamed x5, local copies, waits for them, and re-layouts  12.6 us

profile of v2, /device:TPU:0, one launch (start us, length us, event | category | flops | bytes accessed | tf_op | source)
XLA Modules:
  0.0 235.0 jit_solution(16876543656925151341)
XLA Ops:
  0.6 1.3 copy.7.len_ref
  1.9 221.7 %grads.1 = (f32[1,512,4096]{2,1,0:T(8,128)}, f32[1,2048,1024]{2,1,0:T(8,128)}) custom-call(bf16[4,512,1024]{2,1,0:T(8,128)(2,1)} %x_hbm.1, bf16[4,512,1024]{2,1,0:T(8,128)(2,1)} %dy_hbm.1, s32[4,1]{1,0:T(4,128)} %copy.7.len_ref, bf16[1,512,4096]{2,1,0:T(8,128)(2,1)} %wu_hbm.1, bf16[1,2048,1024]{2,1,0:T(8,128)(2,1)} %wd_hbm.1), custom_call_target="tpu_custom_call" | custom-call | tf_op jit(solution)/shard_map/grads/pallas_call | solution.py:394
  223.7 0.0 copy-start
  223.7 7.9 %copy.10 = f32[1,512,4096]{2,1,0:T(8,128)} copy(f32[1,512,4096]{2,1,0:T(8,128)} %get-tuple-element.4) | data formatting | bytes 16777216
  231.6 0.0 copy-done
  231.6 3.4 %copy.11 = f32[1,2048,1024]{2,1,0:T(8,128)} copy(f32[1,2048,1024]{2,1,0:T(8,128)S(1)} %copy-done) | data formatting | bytes 16777216
Async XLA Ops:
  223.7 7.9 %copy-start = (f32[1,2048,1024]{2,1,0:T(8,128)S(1)}, f32[1,2048,1024]{2,1,0:T(8,128)}, u32[]{:S(2)}) copy-start(f32[1,2048,1024]{2,1,0:T(8,128)} %get-tuple-element.5) | copy-start | bytes 25165828
